TPU v7x, 8 devices: a whole 2x2x1 slice. The times are simulated.
8 devices in a mesh: fsdp: 2 (over z, y), model: 4 (over x, core).
Axes of the slice: x: 2, y: 2, z: 1, core: 2. Of those that a mesh axis runs over, the one named last changes fastest.
Arguments:
- x_in: bfloat16 [4, 1024, 3584], P('fsdp', 'model')
- dy_in: bfloat16 [4, 1024, 3584], P('fsdp', 'model')
- norm_gain: float32 [3584], replicated
- w_qkv: bfloat16 [3584, 4608], P('fsdp', 'model')
- w_out: bfloat16 [3584, 3584], P('model', 'fsdp')
- w_gate: bfloat16 [3584, 18944], P('fsdp', 'model')
- w_up: bfloat16 [3584, 18944], P('fsdp', 'model')
- w_down: bfloat16 [18944, 3584], P('model', 'fsdp')
- rope_cos: float32 [1024, 64], replicated
- rope_sin: float32 [1024, 64], replicated
Outputs:
- output 1: bfloat16 [4, 1024, 3584], P('fsdp', 'model')
- output 2: bfloat16 [4, 1024, 3584], P('fsdp', 'model')
- output 3: float32 [3584, 4608], P('fsdp', 'model')
- output 4: float32 [3584, 3584], P('model', 'fsdp')
- output 5: float32 [3584, 18944], P('fsdp', 'model')
- output 6: float32 [3584, 18944], P('fsdp', 'model')
- output 7: float32 [18944, 3584], P('model', 'fsdp')
All inputs are finite; a program needn't handle non-finite values.
Results may differ from a plain program's by a relative error of at most 0.00910455.
Values are sent between devices in bfloat16 or wider.
A program may use at most 1 GiB of HBM per device.

v0:
```python
import jax
import jax.numpy as jnp
from jax import lax
from jax.sharding import PartitionSpec as P, NamedSharding

NORM_EPS = 1e-5


def norm_fwd(row_vals, norm_gain):
    return row_vals * lax.rsqrt(jnp.mean(row_vals * row_vals, axis=-1, keepdims=True) + NORM_EPS) * norm_gain


def swiglu(gate_val, up_val):
    return (jax.nn.silu(gate_val.astype(jnp.float32)) * up_val.astype(jnp.float32)).astype(jnp.bfloat16)


def rotate(tensor, cos_tab, sin_tab):
    half_dim = tensor.shape[-1] // 2
    wide = tensor.astype(jnp.float32)
    lower_half = wide[..., :half_dim]
    upper_half = wide[..., half_dim:]
    return jnp.concatenate([lower_half * cos_tab - upper_half * sin_tab, upper_half * cos_tab + lower_half * sin_tab], axis=-1).astype(jnp.bfloat16)


def attention(qkv_val, rope_cos, rope_sin):
    batch_loc, seq_len, kv_loc, slot_count, head_dim = qkv_val.shape
    group_size = slot_count - 2
    queries = rotate(qkv_val[:, :, :, :group_size, :], rope_cos[None, :, None, None, :], rope_sin[None, :, None, None, :])
    key_rot = rotate(qkv_val[:, :, :, group_size, :], rope_cos[None, :, None, :], rope_sin[None, :, None, :])
    values = qkv_val[:, :, :, group_size + 1, :]
    scores = jnp.einsum("bqkgh,bpkh->bkgqp", queries, key_rot, preferred_element_type=jnp.float32) * head_dim ** -0.5
    causal = jnp.arange(seq_len)[:, None] >= jnp.arange(seq_len)[None, :]
    attn_probs = jax.nn.softmax(jnp.where(causal, scores, -1e30), axis=-1).astype(jnp.bfloat16)
    attn_out = jnp.einsum("bkgqp,bpkh->bqkgh", attn_probs, values, preferred_element_type=jnp.float32)
    return attn_out.astype(jnp.bfloat16).reshape(batch_loc, seq_len, kv_loc * group_size * head_dim)


def solution(mesh):
    act_spec = P("fsdp", "model", None)
    col_spec = P("fsdp", "model")
    row_spec = P("model", "fsdp")

    def layer_body(x_in, dy_in, norm_gain, w_qkv, w_out, w_gate, w_up, w_down, rope_cos, rope_sin):
        full_qkv = lax.all_gather(w_qkv, "fsdp", axis=0, tiled=True)
        full_out = lax.all_gather(w_out, "fsdp", axis=1, tiled=True)
        full_gate = lax.all_gather(w_gate, "fsdp", axis=0, tiled=True)
        full_up = lax.all_gather(w_up, "fsdp", axis=0, tiled=True)
        full_down = lax.all_gather(w_down, "fsdp", axis=1, tiled=True)
        x_rows = x_in.astype(jnp.float32)
        normed, norm_pull = jax.vjp(lambda row_vals: norm_fwd(row_vals, norm_gain), x_rows)
        h_full = lax.all_gather(normed.astype(jnp.bfloat16), "model", axis=1, tiled=True)
        batch_loc = h_full.shape[0]
        seq_len = h_full.shape[1]
        head_dim = 2 * rope_cos.shape[1]
        heads_loc = w_out.shape[0] // head_dim
        kv_loc = (w_qkv.shape[1] // head_dim - heads_loc) // 2
        qkv_val = jnp.einsum("bsd,dc->bsc", h_full, full_qkv, preferred_element_type=jnp.float32).astype(jnp.bfloat16)
        qkv_heads = qkv_val.reshape(batch_loc, seq_len, kv_loc, heads_loc // kv_loc + 2, head_dim)
        attn_val, attn_pull = jax.vjp(lambda packed: attention(packed, rope_cos, rope_sin), qkv_heads)
        gate_val = jnp.einsum("bsd,df->bsf", h_full, full_gate, preferred_element_type=jnp.float32).astype(jnp.bfloat16)
        up_val = jnp.einsum("bsd,df->bsf", h_full, full_up, preferred_element_type=jnp.float32).astype(jnp.bfloat16)
        act_val, act_pull = jax.vjp(swiglu, gate_val, up_val)
        part_sum = jnp.einsum("bsc,cd->bsd", attn_val, full_out, preferred_element_type=jnp.float32) + jnp.einsum("bsf,fd->bsd", act_val, full_down, preferred_element_type=jnp.float32)
        mix_sum = lax.psum_scatter(part_sum, "model", scatter_dimension=1, tiled=True)
        y_out = (x_rows + mix_sum).astype(jnp.bfloat16)
        dy_full = lax.all_gather(dy_in, "model", axis=1, tiled=True)
        dw_out = jnp.einsum("bsc,bsd->cd", attn_val, dy_full, preferred_element_type=jnp.float32)
        dw_down = jnp.einsum("bsf,bsd->fd", act_val, dy_full, preferred_element_type=jnp.float32)
        d_attn = jnp.einsum("bsd,cd->bsc", dy_full, full_out, preferred_element_type=jnp.float32).astype(jnp.bfloat16)
        d_act = jnp.einsum("bsd,fd->bsf", dy_full, full_down, preferred_element_type=jnp.float32).astype(jnp.bfloat16)
        d_qkv = attn_pull(d_attn)[0].reshape(batch_loc, seq_len, -1)
        d_gate, d_up = act_pull(d_act)
        dw_qkv = jnp.einsum("bsd,bsc->dc", h_full, d_qkv, preferred_element_type=jnp.float32)
        dw_gate = jnp.einsum("bsd,bsf->df", h_full, d_gate, preferred_element_type=jnp.float32)
        dw_up = jnp.einsum("bsd,bsf->df", h_full, d_up, preferred_element_type=jnp.float32)
        dh_part = jnp.einsum("bsc,dc->bsd", d_qkv, full_qkv, preferred_element_type=jnp.float32) + jnp.einsum("bsf,df->bsd", d_gate, full_gate, preferred_element_type=jnp.float32) + jnp.einsum("bsf,df->bsd", d_up, full_up, preferred_element_type=jnp.float32)
        d_h = lax.psum_scatter(dh_part, "model", scatter_dimension=1, tiled=True).astype(jnp.bfloat16)
        dx_out = (dy_in.astype(jnp.float32) + norm_pull(d_h.astype(jnp.float32))[0]).astype(jnp.bfloat16)
        return (
            y_out,
            dx_out,
            lax.psum_scatter(dw_qkv, "fsdp", scatter_dimension=0, tiled=True),
            lax.psum_scatter(dw_out, "fsdp", scatter_dimension=1, tiled=True),
            lax.psum_scatter(dw_gate, "fsdp", scatter_dimension=0, tiled=True),
            lax.psum_scatter(dw_up, "fsdp", scatter_dimension=0, tiled=True),
            lax.psum_scatter(dw_down, "fsdp", scatter_dimension=1, tiled=True),
        )

    return jax.shard_map(
        layer_body,
        mesh=mesh,
        in_specs=(act_spec, act_spec, P(), col_spec, row_spec, col_spec, col_spec, row_spec, P(), P()),
        out_specs=(act_spec, act_spec, col_spec, row_spec, col_spec, col_spec, row_spec),
        check_vma=False,
    )
```

profile of v0, /device:TPU:0, one launch (start us, length us, event | category | flops | bytes accessed | tf_op | source)
XLA Modules:
  0.0 4807.0 jit_solution(23775236724062695)
XLA Ops:
  21.1 92.0 %all-gather.10.cloned.1.call-done = bf16[3584,1152]{1,0:T(8,128)(2,1)} async-done(((bf16[1792,1152]{1,0:T(8,128)(2,1)}), bf16[3584,1152]{1,0:T(8,128)(2,1)}) %all-gather.10.cloned.1.call-update) | async-done | bytes 8257552 | tf_op jit(solution)/shard_map/all_gather | solution.py:44
  113.1 94.2 %all-gather.8.cloned.1.call-done = bf16[2,1024,3584]{2,1,0:T(8,128)(2,1)} async-done(((bf16[2,256,3584]{2,1,0:T(8,128)(2,1)}), bf16[2,1024,3584]{2,1,0:T(8,128)(2,1)}) %all-gather.8.cloned.1.call-update) | async-done | bytes 14680080 | tf_op jit(solution)/shard_map/all_gather | solution.py:51
  313.1 69.0 %all-gather.20.cloned.1.call-done = bf16[2,1024,3584]{2,1,0:T(8,128)(2,1)} async-done(((bf16[2,256,3584]{2,1,0:T(8,128)(2,1)}), bf16[2,1024,3584]{2,1,0:T(8,128)(2,1)}) %all-gather.20.cloned.1.call-update) | async-done | bytes 14680080 | tf_op jit(solution)/shard_map/all_gather | solution.py:66
  426.0 38.2 fusion.8
  464.2 38.6 fusion.95
  502.9 40.3 bitcast_convert_fusion
  593.1 182.5 %all-gather.14.cloned.1.call-done = bf16[3584,4736]{1,0:T(8,128)(2,1)} async-done(((bf16[1792,4736]{1,0:T(8,128)(2,1)}), bf16[3584,4736]{1,0:T(8,128)(2,1)}) %all-gather.14.cloned.1.call-update) | async-done | bytes 33947664 | tf_op jit(solution)/shard_map/all_gather | solution.py:46
  775.6 84.2 %fusion.38 = bf16[2,1024,4736]{2,1,0:T(8,128)(2,1)} fusion(bf16[2,1024,3584]{2,1,0:T(8,128)(2,1)} %all-gather.8.cloned.1.call-done, bf16[3584,4736]{1,0:T(8,128)(2,1)} %all-gather.14.cloned.1.call-done), kind=kOutput, calls=%fused_computation.60 | convolution fusion | flops 69534482432 | bytes 68026368 | tf_op jit(solution)/shard_map/bsd,df->bsf/dot_general | solution.py:60
  859.8 309.3 %all-gather.16.cloned.1.call-done = bf16[3584,4736]{1,0:T(8,128)(2,1)} async-done(((bf16[1792,4736]{1,0:T(8,128)(2,1)}), bf16[3584,4736]{1,0:T(8,128)(2,1)}) %all-gather.16.cloned.1.call-update) | async-done | bytes 33947664 | tf_op jit(solution)/shard_map/all_gather | solution.py:47
  1169.1 84.4 %fusion.41 = bf16[2,1024,4736]{2,1,0:T(8,128)(2,1)} fusion(bf16[2,1024,3584]{2,1,0:T(8,128)(2,1)} %all-gather.8.cloned.1.call-done, bf16[3584,4736]{1,0:T(8,128)(2,1)} %all-gather.16.cloned.1.call-done), kind=kOutput, calls=%fused_computation.61 | convolution fusion | flops 69534482432 | bytes 68026368 | tf_op jit(solution)/shard_map/bsd,df->bsf/dot_general | solution.py:61
  1253.5 309.2 %all-gather.18.cloned.1.call-done = bf16[4736,3584]{1,0:T(8,128)(2,1)} async-done(((bf16[4736,1792]{1,0:T(8,128)(2,1)}), bf16[4736,3584]{1,0:T(8,128)(2,1)}) %all-gather.18.cloned.1.call-update) | async-done | bytes 33947664 | tf_op jit(solution)/shard_map/all_gather | solution.py:48
  1562.7 83.5 %fusion.44 = bf16[2,1024,4736]{2,1,0:T(8,128)(2,1)} fusion(bf16[2,1024,3584]{2,1,0:T(8,128)(2,1)} %all-gather.20.cloned.1.call-done, bf16[4736,3584]{1,0:T(8,128)(2,1)} %all-gather.18.cloned.1.call-done), kind=kOutput, calls=%fused_computation.62 | convolution fusion | flops 69534482432 | bytes 68026368 | tf_op jit(solution)/shard_map/bsd,fd->bsf/dot_general | solution.py:70
  1646.2 31.5 fusion.153
  1677.7 96.4 %fusion.22 = f32[2,1024,3584]{2,1,0:T(8,128)} fusion(bf16[3584,4736]{1,0:T(8,128)(2,1)} %all-gather.16.cloned.1.call-done, bf16[2,1024,4736]{2,1,0:T(8,128)(2,1)} %fusion.44, bf16[2,1024,4736]{2,1,0:T(8,128)(2,1)} %fusion.38), kind=kOutput, calls=%fused_computation.37 | convolution fusion | flops 69602377728 | bytes 102105088 | tf_op jit(solution)/shard_map/bsf,df->bsd/dot_general | solution.py:76
  1774.1 90.8 %add_add_fusion = f32[2,1024,3584]{2,1,0:T(8,128)} fusion(f32[2,1024,3584]{2,1,0:T(8,128)} %fusion.22, f32[2,1024,3584]{2,1,0:T(8,128)} %fusion.49, bf16[3584,4736]{1,0:T(8,128)(2,1)} %all-gather.14.cloned.1.call-done, bf16[2,1024,4736]{2,1,0:T(8,128)(2,1)} %fusion.153), kind=kOutput, calls=%fused_computation.49 | convolution fusion | flops 69539463168 | bytes 141426688 | tf_op jit(solution)/shard_map/bsf,df->bsd/dot_general | solution.py:76
  1891.1 89.4 %fusion.20 = f32[2,1024,3584]{2,1,0:T(8,128)} fusion(bf16[4736,3584]{1,0:T(8,128)(2,1)} %all-gather.18.cloned.1.call-done, bf16[2,1024,4736]{2,1,0:T(8,128)(2,1)} %fusion.41, bf16[2,1024,4736]{2,1,0:T(8,128)(2,1)} %fusion.38), kind=kOutput, calls=%fused_computation.35 | convolution fusion | flops 69602377728 | bytes 102105088 | tf_op jit(solution)/shard_map/bsf,fd->bsd/dot_general | solution.py:63
  2055.8 89.8 %convolution_bitcast_fusion.1 = f32[3584,4736]{1,0:T(8,128)} fusion(bf16[2,1024,3584]{2,1,0:T(8,128)(2,1)} %all-gather.8.cloned.1.call-done, bf16[2,1024,4736]{2,1,0:T(8,128)(2,1)} %fusion.38, bf16[2,1024,4736]{2,1,0:T(8,128)(2,1)} %fusion.41, bf16[2,1024,4736]{2,1,0:T(8,128)(2,1)} %fusion.44), kind=kOutput, calls=%fused_computation.23 | convolution fusion | flops 69660573696 | bytes 140771328 | tf_op jit(solution)/shard_map/bsd,bsf->df/dot_general | solution.py:74
  2145.6 88.2 %convolution_bitcast_fusion = f32[3584,4736]{1,0:T(8,128)} fusion(bf16[2,1024,3584]{2,1,0:T(8,128)(2,1)} %all-gather.8.cloned.1.call-done, bf16[2,1024,4736]{2,1,0:T(8,128)(2,1)} %fusion.44, bf16[2,1024,4736]{2,1,0:T(8,128)(2,1)} %fusion.38), kind=kOutput, calls=%fused_computation.22 | convolution fusion | flops 69602377728 | bytes 121372672 | tf_op jit(solution)/shard_map/bsd,bsf->df/dot_general | solution.py:75
  2233.8 86.1 %convolution_bitcast_fusion.2 = f32[4736,3584]{1,0:T(8,128)} fusion(bf16[2,1024,3584]{2,1,0:T(8,128)(2,1)} %all-gather.20.cloned.1.call-done, bf16[2,1024,4736]{2,1,0:T(8,128)(2,1)} %fusion.41, bf16[2,1024,4736]{2,1,0:T(8,128)(2,1)} %fusion.38), kind=kOutput, calls=%fused_computation.24 | convolution fusion | flops 69602377728 | bytes 121372672 | tf_op jit(solution)/shard_map/bsf,bsd->fd/dot_general | solution.py:68
  2338.0 65.3 %reduce-scatter.14.cloned.1.call-done = f32[896,1792]{1,0:T(8,128)} async-done(((f32[896,3584]{1,0:T(8,128)}), f32[896,1792]{1,0:T(8,128)}) %reduce-scatter.14.cloned.1.call-update) | async-done | bytes 6422544 | tf_op jit(solution)/shard_map/reduce_scatter | solution.py:83
  2403.4 186.4 %reduce-scatter.12.cloned.1.call-done = f32[1792,1152]{1,0:T(8,128)} async-done(((f32[3584,1152]{1,0:T(8,128)}), f32[1792,1152]{1,0:T(8,128)}) %reduce-scatter.12.cloned.1.call-update) | async-done | bytes 8257552 | tf_op jit(solution)/shard_map/reduce_scatter | solution.py:82
  2589.8 736.8 %reduce-scatter.16.cloned.1.call-done = f32[1792,4736]{1,0:T(8,128)} async-done(((f32[3584,4736]{1,0:T(8,128)}), f32[1792,4736]{1,0:T(8,128)}) %reduce-scatter.16.cloned.1.call-update) | async-done | bytes 33947664 | tf_op jit(solution)/shard_map/reduce_scatter | solution.py:84
  3326.6 736.9 %reduce-scatter.18.cloned.1.call-done = f32[1792,4736]{1,0:T(8,128)} async-done(((f32[3584,4736]{1,0:T(8,128)}), f32[1792,4736]{1,0:T(8,128)}) %reduce-scatter.18.cloned.1.call-update) | async-done | bytes 33947664 | tf_op jit(solution)/shard_map/reduce_scatter | solution.py:85
  4063.5 736.8 %reduce-scatter.20.cloned.1.call-done = f32[4736,1792]{1,0:T(8,128)} async-done(((f32[4736,3584]{1,0:T(8,128)}), f32[4736,1792]{1,0:T(8,128)}) %reduce-scatter.20.cloned.1.call-update) | async-done | bytes 33947664 | tf_op jit(solution)/shard_map/reduce_scatter | solution.py:86
  (107 shorter events, 332.9 us)
Async XLA Ops:
  7.2 105.9 %all-gather.10.cloned.1.call-start = ((), (), s32[]{:S(2)}) async-start(), calls=%async_computation.8 | async-start | bytes 12386304 | tf_op jit(solution)/shard_map/all_gather | solution.py:44
  7.9 199.4 %all-gather.8.cloned.1.call-start = ((), (), s32[]{:S(2)}) async-start(), calls=%async_computation.7 | async-start | bytes 18350080 | tf_op jit(solution)/shard_map/all_gather | solution.py:51
  17.1 296.1 %all-gather.12.cloned.1.call-start = ((), (), s32[]{:S(2)}) async-start(), calls=%async_computation.9 | async-start | bytes 9633792 | tf_op jit(solution)/shard_map/all_gather | solution.py:45
  17.8 364.3 %all-gather.20.cloned.1.call-start = ((), (), s32[]{:S(2)}) async-start(), calls=%async_computation.14 | async-start | bytes 18350080 | tf_op jit(solution)/shard_map/all_gather | solution.py:66
  18.4 757.2 %all-gather.14.cloned.1.call-start = ((), (), s32[]{:S(2)}) async-start(), calls=%async_computation.10 | async-start | bytes 50921472 | tf_op jit(solution)/shard_map/all_gather | solution.py:46
  19.0 1150.1 %all-gather.16.cloned.1.call-start = ((), (), s32[]{:S(2)}) async-start(), calls=%async_computation.11 | async-start | bytes 50921472 | tf_op jit(solution)/shard_map/all_gather | solution.py:47
  19.6 1543.2 %all-gather.18.cloned.1.call-start = ((), (), s32[]{:S(2)}) async-start(), calls=%async_computation.12 | async-start | bytes 50921472 | tf_op jit(solution)/shard_map/all_gather | solution.py:48
  20.3 2299.7 %reduce-scatter.10.cloned.1.call-start = ((), (), s32[]{:S(2)}) async-start(), calls=%async_computation.15 | async-start | bytes 36700160 | tf_op jit(solution)/shard_map/reduce_scatter | solution.py:77
  20.7 482.1 %copy-start = (pred[1024,1024]{0,1:T(8,128)(4,1)}, pred[1024,1024]{0,1:T(8,128)(4,1)S(1)}, u32[]{:S(2)}) copy-start(pred[1024,1024]{0,1:T(8,128)(4,1)S(1)} %iota_compare_fusion) | copy-start | bytes 3145732
  20.9 244.2 %copy-start.2 = (f32[1024,64]{1,0:T(8,128)}, f32[1024,64]{1,0:T(8,128)S(1)}, u32[]{:S(2)}) copy-start(f32[1024,64]{1,0:T(8,128)S(1)} %copy.40) | copy-start | bytes 786436
  21.1 244.0 %copy-start.4 = (f32[1024,64]{1,0:T(8,128)}, f32[1024,64]{1,0:T(8,128)S(1)}, u32[]{:S(2)}) copy-start(f32[1024,64]{1,0:T(8,128)S(1)} %copy.41) | copy-start | bytes 786436
  265.5 28.2 copy-start.6
  265.6 28.2 copy-start.7
  293.7 209.1 %copy-start.13 = (f32[2,7,1024]{2,1,0:T(8,128)}, f32[2,7,1024]{2,1,0:T(8,128)S(1)}, u32[]{:S(2)}) copy-start(f32[2,7,1024]{2,1,0:T(8,128)S(1)} %get-tuple-element.17) | copy-start | bytes 172036
  313.1 189.8 %copy-start.9 = (f32[2,7,1024]{2,1,0:T(8,128)}, f32[2,7,1024]{2,1,0:T(8,128)S(1)}, u32[]{:S(2)}) copy-start(f32[2,7,1024]{2,1,0:T(8,128)S(1)} %fusion.76) | copy-start | bytes 172036
  502.8 40.3 copy-start.3
  502.8 40.3 copy-start.5
  543.6 13.7 copy-start.8
  1865.0 461.0 %reduce-scatter.8.cloned.1.call-start = ((), (), s32[]{:S(2)}) async-start(), calls=%async_computation.13 | async-start | bytes 36700160 | tf_op jit(solution)/shard_map/reduce_scatter | solution.py:64
  2009.5 393.9 %reduce-scatter.14.cloned.1.call-start = ((), (), s32[]{:S(2)}) async-start(), calls=%async_computation.17 | async-start | bytes 19267584 | tf_op jit(solution)/shard_map/reduce_scatter | solution.py:83
  2030.0 559.8 %reduce-scatter.12.cloned.1.call-start = ((), (), s32[]{:S(2)}) async-start(), calls=%async_computation.16 | async-start | bytes 24772608 | tf_op jit(solution)/shard_map/reduce_scatter | solution.py:82
  2055.7 1270.9 %reduce-scatter.16.cloned.1.call-start = ((), (), s32[]{:S(2)}) async-start(), calls=%async_computation.18 | async-start | bytes 101842944 | tf_op jit(solution)/shard_map/reduce_scatter | solution.py:84
  2145.5 1918.0 %reduce-scatter.18.cloned.1.call-start = ((), (), s32[]{:S(2)}) async-start(), calls=%async_computation.19 | async-start | bytes 101842944 | tf_op jit(solution)/shard_map/reduce_scatter | solution.py:85
  2233.8 2566.5 %reduce-scatter.20.cloned.1.call-start = ((), (), s32[]{:S(2)}) async-start(), calls=%async_computation.20 | async-start | bytes 101842944 | tf_op jit(solution)/shard_map/reduce_scatter | solution.py:86
  (10 other events, 21.2 us)
Sparse Core Ops, SparseCore 0:
  9.5 103.5 all-gather.9
  115.2 92.0 all-gather.7
  208.8 79.7 all-gather.11
  290.0 92.0 all-gather.19
  383.5 392.0 all-gather.13
  777.0 392.0 all-gather.15
  1170.6 392.0 all-gather.17
  1865.1 194.2 reduce-scatter.9
  2061.9 194.1 reduce-scatter.7
  2258.8 144.4 reduce-scatter.13
  2406.3 183.5 reduce-scatter.11
  2592.5 734.0 reduce-scatter.15
  3329.4 734.0 reduce-scatter.17
  4066.2 734.0 reduce-scatter.19
where the time goes:
time: 4820 us; the launch traced here: 4810 us
  waiting for transfers between devices  3520 us (73%)
  matrix products  1130 us (23%)
  other arithmetic  108 us (2%)
    reduce_scatter x1, waiting for transfers between devices, layer_body(): lax.psum_scatter(dw_up, 'fsdp', scatter_dimension=0, tiled=True)  737 us
    reduce_scatter x1, waiting for transfers between devices, layer_body(): lax.psum_scatter(dw_down, 'fsdp', scatter_dimension=1, tiled=True)  737 us
    reduce_scatter x1, waiting for transfers between devices, layer_body(): lax.psum_scatter(dw_gate, 'fsdp', scatter_dimension=0, tiled=True)  737 us
    all_gather x1, waiting for transfers between devices, layer_body(): full_up = lax.all_gather(w_up, 'fsdp', axis=0, tiled=True)  309 us
    all_gather x1, waiting for transfers between devices, layer_body(): full_down = lax.all_gather(w_down, 'fsdp', axis=1, tiled=True)  309 us
    reduce_scatter x1, waiting for transfers between devices, layer_body(): lax.psum_scatter(dw_qkv, 'fsdp', scatter_dimension=0, tiled=True)  186 us
    all_gather x1, waiting for transfers between devices, layer_body(): full_gate = lax.all_gather(w_gate, 'fsdp', axis=0, tiled=True)  183 us
    dot_general x3, matrix products, attention(): jnp.einsum('bqkgh,bpkh->bkgqp', queries, key_rot, preferred_element_type=...  107 us
  transfers between devices with their start and end apart: 14, of which 11 were waited for; matrix products, arithmetic and copies ran while one was open for 20% of the time, Pallas kernels for 0%

commit v1 on v0

v1 whole, which is shorter than its diff:
```python
import functools

import jax
import jax.numpy as jnp
from jax import lax
from jax.experimental import pallas as pl
from jax.experimental.pallas import tpu as pltpu
from jax.sharding import PartitionSpec as P


NORM_EPS = 1e-5
ROW_BLOCK = 256
CUT_LANES, CUT_TOTAL = 19, 37


def norm_fwd(row_vals, norm_gain):
    return row_vals * lax.rsqrt(jnp.mean(row_vals * row_vals, axis=-1, keepdims=True) + NORM_EPS) * norm_gain


def swiglu(gate_val, up_val):
    return (jax.nn.silu(gate_val.astype(jnp.float32)) * up_val.astype(jnp.float32)).astype(jnp.bfloat16)


def dot_nn(lhs, rhs):
    return lax.dot_general(lhs, rhs, (((1,), (0,)), ((), ())), preferred_element_type=jnp.float32)


def dot_nt(lhs, rhs):
    return lax.dot_general(lhs, rhs, (((1,), (1,)), ((), ())), preferred_element_type=jnp.float32)


def dot_tn(lhs, rhs):
    return lax.dot_general(lhs, rhs, (((0,), (0,)), ((), ())), preferred_element_type=jnp.float32)


def after(value, *earlier):
    return lax.optimization_barrier((value, earlier))[0]


def attention_kernel(group_size, q_ref, k_ref, v_ref, do_ref, cos_ref, sin_ref, o_ref, dqkv_ref, k_rot, dk_acc, dv_acc):
    head = pl.program_id(1)
    seq_len, head_dim = q_ref.shape
    scale = head_dim ** -0.5

    def turn(tensor, sign):
        wide = tensor.astype(jnp.float32)
        return (wide * cos_ref[...] + pltpu.roll(wide, head_dim // 2, 1) * (sin_ref[...] * sign)).astype(jnp.bfloat16)

    @pl.when(head == 0)
    def _():
        k_rot[...] = turn(k_ref[...], 1.0)
        dk_acc[...] = jnp.zeros_like(dk_acc)
        dv_acc[...] = jnp.zeros_like(dv_acc)

    q_rot = turn(q_ref[...], 1.0)
    dq_blocks = []
    for block in range(seq_len // ROW_BLOCK):
        rows = slice(block * ROW_BLOCK, (block + 1) * ROW_BLOCK)
        width = (block + 1) * ROW_BLOCK
        q_blk = q_rot[rows, :]
        do_blk = do_ref[rows, :]
        scores = dot_nt(q_blk, k_rot[:width, :]) * scale
        row_pos = lax.broadcasted_iota(jnp.int32, (ROW_BLOCK, width), 0) + block * ROW_BLOCK
        col_pos = lax.broadcasted_iota(jnp.int32, (ROW_BLOCK, width), 1)
        scores = jnp.where(row_pos >= col_pos, scores, -1e30)
        weights = jnp.exp(scores - jnp.max(scores, axis=-1, keepdims=True))
        probs = weights / jnp.sum(weights, axis=-1, keepdims=True)
        probs_b = probs.astype(jnp.bfloat16)
        o_ref[rows, :] = dot_nn(probs_b, v_ref[:width, :]).astype(jnp.bfloat16)
        d_probs = dot_nt(do_blk, v_ref[:width, :]).astype(jnp.bfloat16).astype(jnp.float32)
        inner = jnp.sum(probs * d_probs, axis=-1, keepdims=True)
        d_scores = (probs * (d_probs - inner) * scale).astype(jnp.bfloat16)
        dq_blocks.append(dot_nn(d_scores, k_rot[:width, :]))
        dk_acc[:width, :] += dot_tn(d_scores, q_blk)
        dv_acc[:width, :] += dot_tn(probs_b, do_blk)
    dq = jnp.concatenate(dq_blocks, axis=0).astype(jnp.bfloat16)
    dqkv_ref[:, pl.ds(pl.multiple_of(head * head_dim, head_dim), head_dim)] = turn(dq, -1.0)

    @pl.when(head == group_size - 1)
    def _():
        dqkv_ref[:, group_size * head_dim:(group_size + 1) * head_dim] = turn(dk_acc[...].astype(jnp.bfloat16), -1.0)
        dqkv_ref[:, (group_size + 1) * head_dim:] = dv_acc[...].astype(jnp.bfloat16)


def attention_grads(qkv_val, d_attn, rope_cos, rope_sin, seq_len):
    tokens, qkv_cols = qkv_val.shape
    head_dim = 2 * rope_cos.shape[1]
    group_size = d_attn.shape[1] // head_dim
    seqs = tokens // seq_len
    cos_full = jnp.concatenate([rope_cos, rope_cos], axis=1)
    sin_full = jnp.concatenate([-rope_sin, rope_sin], axis=1)
    head_spec = pl.BlockSpec((seq_len, head_dim), lambda s, h: (s, h))
    table_spec = pl.BlockSpec((seq_len, head_dim), lambda s, h: (0, 0))
    return pl.pallas_call(
        functools.partial(attention_kernel, group_size),
        grid=(seqs, group_size),
        in_specs=[
            head_spec,
            pl.BlockSpec((seq_len, head_dim), lambda s, h: (s, group_size)),
            pl.BlockSpec((seq_len, head_dim), lambda s, h: (s, group_size + 1)),
            head_spec,
            table_spec,
            table_spec,
        ],
        out_specs=[head_spec, pl.BlockSpec((seq_len, qkv_cols), lambda s, h: (s, 0))],
        out_shape=[
            jax.ShapeDtypeStruct(d_attn.shape, jnp.bfloat16),
            jax.ShapeDtypeStruct(qkv_val.shape, jnp.bfloat16),
        ],
        scratch_shapes=[
            pltpu.VMEM((seq_len, head_dim), jnp.bfloat16),
            pltpu.VMEM((seq_len, head_dim), jnp.float32),
            pltpu.VMEM((seq_len, head_dim), jnp.float32),
        ],
        compiler_params=pltpu.CompilerParams(dimension_semantics=("arbitrary", "arbitrary"), vmem_limit_bytes=40 * 2**20),
        cost_estimate=pl.CostEstimate(flops=seqs * group_size * seq_len * seq_len * head_dim * 24, bytes_accessed=2 * 2 * (qkv_val.size + d_attn.size), transcendentals=seqs * group_size * seq_len * seq_len),
        name="attention_grads",
    )(qkv_val, qkv_val, qkv_val, d_attn, cos_full, sin_full)


def solution(mesh):
    act_spec = P("fsdp", "model", None)
    col_spec = P("fsdp", "model")
    row_spec = P("model", "fsdp")

    def swap(value):
        return lax.ppermute(value, "fsdp", [(0, 1), (1, 0)])

    def layer_body(x_in, dy_in, norm_gain, w_qkv, w_out, w_gate, w_up, w_down, rope_cos, rope_sin):
        me = lax.axis_index("fsdp")
        half = w_qkv.shape[0]
        batch_loc = x_in.shape[0]
        seq_len = rope_cos.shape[0]
        ffn = w_gate.shape[1]

        def halves(value):
            return [lax.dynamic_slice_in_dim(value, side * half, half, axis=2) for side in (me, 1 - me)]

        def join(own, other):
            return jnp.where(me == 0, jnp.concatenate([own, other], axis=2), jnp.concatenate([other, own], axis=2))

        def all_tokens(value):
            own, other = halves(value)
            peer_own = swap(other)
            peer_other = swap(own)
            full_own = lax.all_gather(jnp.concatenate([own, peer_own], axis=0), "model", axis=1, tiled=True)
            full_other = lax.all_gather(jnp.concatenate([other, peer_other], axis=0), "model", axis=1, tiled=True)
            return full_own.reshape(-1, half), full_other.reshape(-1, half)

        x_rows = x_in.astype(jnp.float32)
        normed, norm_pull = jax.vjp(lambda row_vals: norm_fwd(row_vals, norm_gain), x_rows)
        h_own, h_oth = all_tokens(normed.astype(jnp.bfloat16))
        dy_own, dy_oth = all_tokens(dy_in)
        cut = CUT_LANES * (ffn // CUT_TOTAL)
        weights = {
            "wqkv": w_qkv, "wout": w_out,
            "gate0": w_gate[:, :cut], "up0": w_up[:, :cut], "down0": w_down[:cut, :],
            "gate1": w_gate[:, cut:], "up1": w_up[:, cut:], "down1": w_down[cut:, :],
        }
        peers = {}
        for name, weight in weights.items():
            peers[name] = swap(weight)

        gate0_own = dot_nn(h_own, weights["gate0"])
        up0_own = dot_nn(h_own, weights["up0"])
        qkv_val = (dot_nn(h_own, w_qkv) + dot_nn(h_oth, after(peers["wqkv"], gate0_own, up0_own))).astype(jnp.bfloat16)
        h_late = after(h_own, qkv_val)
        gate1_own = dot_nn(h_late, weights["gate1"])
        up1_own = dot_nn(h_late, weights["up1"])
        dy_late = after(dy_own, gate1_own, up1_own)
        down0_own = dot_nt(dy_late, weights["down0"])
        d_attn = (dot_nt(dy_late, w_out) + dot_nt(dy_oth, after(peers["wout"], down0_own))).astype(jnp.bfloat16)
        attn_val, d_qkv = attention_grads(qkv_val, d_attn, rope_cos, rope_sin, seq_len)

        gate0 = (gate0_own + dot_nn(h_oth, after(peers["gate0"], d_qkv))).astype(jnp.bfloat16)
        attn_late, d_qkv_late = after((attn_val, d_qkv), gate0)
        part_sum = dot_nn(attn_late, w_out)
        dh_part = dot_nt(d_qkv_late, w_qkv)
        dw_out = dot_tn(attn_late, dy_own)
        dw_qkv = dot_tn(h_own, d_qkv_late)
        up0 = (up0_own + dot_nn(h_oth, after(peers["up0"], part_sum, dh_part, dw_out, dw_qkv))).astype(jnp.bfloat16)
        act0, act0_pull = jax.vjp(swiglu, gate0, up0)
        part_sum = part_sum + dot_nn(act0, weights["down0"])
        dw_down0 = dot_tn(act0, dy_own)
        down1_own = dot_nt(after(dy_own, part_sum, dw_down0), weights["down1"])
        d_act0 = (down0_own + dot_nt(dy_oth, after(peers["down0"], down1_own))).astype(jnp.bfloat16)
        d_gate0, d_up0 = act0_pull(d_act0)
        dh_part = dh_part + dot_nt(d_gate0, weights["gate0"]) + dot_nt(d_up0, weights["up0"])

        gate1 = (gate1_own + dot_nn(h_oth, after(peers["gate1"], dh_part))).astype(jnp.bfloat16)
        up1 = (up1_own + dot_nn(h_oth, after(peers["up1"], gate1))).astype(jnp.bfloat16)
        act1, act1_pull = jax.vjp(swiglu, gate1, up1)
        part_sum = part_sum + dot_nn(act1, weights["down1"])
        act_late = after((act0, act1), part_sum)
        dw_down = dot_tn(jnp.concatenate(act_late, axis=1), dy_own)
        d_act1 = (down1_own + dot_nt(dy_oth, after(peers["down1"], dw_down))).astype(jnp.bfloat16)
        d_gate1, d_up1 = act1_pull(d_act1)
        mix_sum = lax.psum_scatter(part_sum.reshape(2 * batch_loc, seq_len, half), "model", scatter_dimension=1, tiled=True)
        mid = batch_loc * seq_len
        gate1_late, up1_late = after((weights["gate1"], weights["up1"]), mix_sum)
        dh_peer = dh_part[mid:] + dot_nt(d_gate1[mid:], gate1_late) + dot_nt(d_up1[mid:], up1_late)
        gate1_late, up1_late = after((gate1_late, up1_late), dh_peer)
        dh_mine = dh_part[:mid] + dot_nt(d_gate1[:mid], gate1_late) + dot_nt(d_up1[:mid], up1_late)
        h_last, gates_last, ups_last = after((h_own, (d_gate0, d_gate1), (d_up0, d_up1)), dh_mine)
        dw_gate = dot_tn(h_last, jnp.concatenate(gates_last, axis=1))
        dw_up = dot_tn(h_last, jnp.concatenate(ups_last, axis=1))

        mix_oth = swap(mix_sum[batch_loc:])
        y_out = (x_rows + join(mix_sum[:batch_loc], mix_oth)).astype(jnp.bfloat16)
        d_h_peer = lax.psum_scatter(dh_peer.reshape(batch_loc, seq_len, half), "model", scatter_dimension=1, tiled=True).astype(jnp.bfloat16)
        d_h_mine = lax.psum_scatter(dh_mine.reshape(batch_loc, seq_len, half), "model", scatter_dimension=1, tiled=True).astype(jnp.bfloat16)
        d_h_oth = swap(d_h_peer)
        d_h = join(d_h_mine, d_h_oth)
        dx_out = (dy_in.astype(jnp.float32) + norm_pull(d_h.astype(jnp.float32))[0]).astype(jnp.bfloat16)
        return (
            y_out,
            dx_out,
            dw_qkv,
            dw_out,
            dw_gate,
            dw_up,
            dw_down,
        )

    return jax.shard_map(
        layer_body,
        mesh=mesh,
        in_specs=(act_spec, act_spec, P(), col_spec, row_spec, col_spec, col_spec, row_spec, P(), P()),
        out_specs=(act_spec, act_spec, col_spec, row_spec, col_spec, col_spec, row_spec),
        check_vma=False,
    )
```

time: 4820 us -> 1910 us (0.40)
  waiting for transfers between devices: 3520 us -> 311 us
  matrix products: 1130 us -> 1330 us
  Pallas kernels: 0 us -> 133 us
  other arithmetic: 108 us -> 35.4 us
    reduce_scatter x7 -> x3, waiting for transfers between devices: 2460 us -> 0.01 us  [the longest x1 0.01 us: layer_body(): lax.psum_scatter(part_sum.reshape(2 * batch_loc, seq_len, half), 'model',...]
    all_gather x7 -> x4, waiting for transfers between devices: 1060 us -> 0.02 us  [the longest x2 0.02 us: all_tokens(): lax.all_gather(jnp.concatenate([own, peer_own], axis=0), 'model', axis=1,...]
    ppermute x0 -> x14, waiting for transfers between devices: none -> 310 us  [swap(): return lax.ppermute(value, 'fsdp', [(0, 1), (1, 0)])]
    dot_general x21 -> x31, matrix products: 1130 us -> 1330 us  [the longest x13 544 us: dot_nn(): lax.dot_general(lhs, rhs, (((1,), (0,)), ((), ())), preferred_element_typ...]
    pallas_call x0 -> x1, Pallas kernels: none -> 133 us  [attention_grads(): pl.pallas_call(functools.partial(attention_kernel, group_size), grid=(seq...]
    slice x2 -> x7, local copies, waits for them, and re-layouts: 5.39 us -> 54.9 us  [the longest x1 9.16 us: layer_body(): w_up[:, :cut]]
  transfers between devices with their start and end apart: 14 -> 21, of which waited for: 11 -> 5; matrix products, arithmetic and copies ran while one was open for 20% -> 66% of each run, Pallas kernels for 0% -> 7%
where the time goes in v1:
time: 1910 us
  matrix products  1330 us (70%)
  waiting for transfers between devices  311 us (16%)
  Pallas kernels  133 us (7%)
  local copies, waits for them, and re-layouts  64 us (3%)
  other arithmetic  35.4 us (2%)
    dot_general x13, matrix products, dot_nn(): lax.dot_general(lhs, rhs, (((1,), (0,)), ((), ())), preferred_element_typ...  544 us
    dot_general x13, matrix products, dot_nt(): lax.dot_general(lhs, rhs, (((1,), (1,)), ((), ())), preferred_element_typ...  485 us
    ppermute x14, waiting for transfers between devices, swap(): return lax.ppermute(value, 'fsdp', [(0, 1), (1, 0)])  310 us
    dot_general x5, matrix products, dot_tn(): lax.dot_general(lhs, rhs, (((0,), (0,)), ((), ())), preferred_element_typ...  304 us
    pallas_call x1, Pallas kernels, attention_grads(): pl.pallas_call(functools.partial(attention_kernel, group_size), grid=(seq...  133 us
  transfers between devices with their start and end apart: 21, of which 5 were waited for; matrix products, arithmetic and copies ran while one was open for 66% of the time, Pallas kernels for 7%

profile of v1, /device:TPU:0, one launch (start us, length us, event | category | flops | bytes accessed | tf_op | source)
XLA Modules:
  0.0 1907.7 jit_solution(1270732745253124673)
XLA Ops:
  18.1 40.0 %collective-permute-done = bf16[2,256,1792]{2,1,0:T(8,128)(2,1)S(1)} collective-permute-done((bf16[2,256,1792]{2,1,0:T(8,128)(2,1)S(1)}, bf16[2,256,1792]{2,1,0:T(8,128)(2,1)S(1)}, u32[]{:S(2)}, u32[]{:S(2)}) %collective-permute-start) | collective-permute-done | bytes 1835040 | tf_op jit(solution)/shard_map/ppermute | solution.py:127
  62.1 39.6 %collective-permute-done.1 = bf16[2,256,1792]{2,1,0:T(8,128)(2,1)S(1)} collective-permute-done((bf16[2,256,1792]{2,1,0:T(8,128)(2,1)}, bf16[2,256,1792]{2,1,0:T(8,128)(2,1)S(1)}, u32[]{:S(2)}, u32[]{:S(2)}) %collective-permute-start.1) | collective-permute-done | bytes 1835040 | tf_op jit(solution)/shard_map/ppermute | solution.py:127
  200.2 46.9 %fusion.65 = f32[4096,2432]{1,0:T(8,128)} fusion(bf16[4096,1792]{1,0:T(8,128)(2,1)} %bitcast.58, bf16[1792,4736]{1,0:T(8,128)(2,1)} %param.16), kind=kOutput, calls=%fused_computation.109 | convolution fusion | flops 35701915648 | bytes 63242240 | tf_op jit(solution)/shard_map/dot_general | solution.py:25
  247.2 47.1 %fusion.69 = f32[4096,2432]{1,0:T(8,128)} fusion(bf16[4096,1792]{1,0:T(8,128)(2,1)} %bitcast.59, bf16[1792,4736]{1,0:T(8,128)(2,1)} %param.15), kind=kOutput, calls=%fused_computation.113 | convolution fusion | flops 35701915648 | bytes 63242240 | tf_op jit(solution)/shard_map/dot_general | solution.py:25
  349.2 45.5 %fusion.54 = f32[4096,2304]{1,0:T(8,128)} fusion(bf16[4096,1792]{1,0:T(8,128)(2,1)} %bitcast.61, bf16[1792,4736]{1,0:T(8,128)(2,1)} %param.16), kind=kOutput, calls=%fused_computation.98 | convolution fusion | flops 33822867456 | bytes 60686336 | tf_op jit(solution)/shard_map/dot_general | solution.py:25
  394.6 43.2 %fusion.56 = f32[4096,2304]{1,0:T(8,128)} fusion(bf16[4096,1792]{1,0:T(8,128)(2,1)} %bitcast.62, bf16[1792,4736]{1,0:T(8,128)(2,1)} %param.15), kind=kOutput, calls=%fused_computation.100 | convolution fusion | flops 33822867456 | bytes 60686336 | tf_op jit(solution)/shard_map/dot_general | solution.py:25
  437.9 46.9 %fusion.62 = f32[4096,2432]{1,0:T(8,128)} fusion(bf16[4096,1792]{1,0:T(8,128)(2,1)} %bitcast.73, bf16[4736,1792]{1,0:T(8,128)(2,1)} %param.17), kind=kOutput, calls=%fused_computation.106 | convolution fusion | flops 35701915648 | bytes 63242240 | tf_op jit(solution)/shard_map/dot_general | solution.py:29
  529.0 133.4 %attention_grads.1 = (bf16[4096,896]{1,0:T(8,128)(2,1)S(1)}, bf16[4096,1152]{1,0:T(8,128)(2,1)}) custom-call(bf16[4096,1152]{1,0:T(8,128)(2,1)} %fusion.28.q_ref.k_ref.v_ref, bf16[4096,1152]{1,0:T(8,128)(2,1)} %fusion.28.q_ref.k_ref.v_ref, bf16[4096,1152]{1,0:T(8,128)(2,1)} %fusion.28.q_ref.k_ref.v_ref, bf16[4096,896]{1,0:T(8,128)(2,1)} %add_convert_fusion.6.do_ref, ...), custom_call_target="tpu_custom_call" | custom-call | flops 90194313216 | bytes 33554432 | tf_op jit(solution)/shard_map/attention_grads/pallas_call | solution.py:94
  665.4 48.4 %add_convert_fusion.2 = bf16[4096,2432]{1,0:T(8,128)(2,1)} fusion(f32[4096,2432]{1,0:T(8,128)} %fusion.69, bf16[4096,1792]{1,0:T(8,128)(2,1)} %bitcast.69, bf16[1792,2432]{1,0:T(8,128)(2,1)} %collective-permute-done.6), kind=kOutput, calls=%fused_computation.24 | convolution fusion | flops 35721838592 | bytes 83165184 | tf_op jit(solution)/shard_map/dot_general | solution.py:25
  804.3 53.2 %fusion = (bf16[4096,2432]{1,0:T(8,128)(2,1)}, bf16[4096,2432]{1,0:T(8,128)(2,1)}) fusion(bf16[4096,2432]{1,0:T(8,128)(2,1)} %add_convert_fusion.2, f32[4096,2432]{1,0:T(8,128)} %fusion.65, bf16[4096,1792]{1,0:T(8,128)(2,1)} %bitcast.70, bf16[1792,2432]{1,0:T(8,128)(2,1)} %collective-permute-done.7), kind=kOutput, calls=%fused_computation.14 | convolution fusion | flops 35801530368 | bytes 123011072 | tf_op jit(solution)/shard_map/dot_general | solution.py:25
  857.5 46.6 %convolution_add_fusion.2 = f32[4096,1792]{1,0:T(8,128)} fusion(f32[4096,1792]{1,0:T(8,128)} %fusion.74, bf16[4096,2432]{1,0:T(8,128)(2,1)} %get-tuple-element.47, bf16[4736,1792]{1,0:T(8,128)(2,1)} %param.17), kind=kOutput, calls=%fused_computation.51 | convolution fusion | flops 35709255680 | bytes 87359488 | tf_op jit(solution)/shard_map/dot_general | solution.py:25
  904.1 43.0 %fusion.59 = f32[4096,2304]{1,0:T(8,128)} fusion(bf16[4096,1792]{1,0:T(8,128)(2,1)} %bitcast.76, bf16[4736,1792]{1,0:T(8,128)(2,1)} %param.17), kind=kOutput, calls=%fused_computation.103 | convolution fusion | flops 33822867456 | bytes 60686336 | tf_op jit(solution)/shard_map/dot_general | solution.py:29
  947.1 62.3 %fusion.1 = (bf16[4096,2432]{1,0:T(8,128)(2,1)}, bf16[4096,2432]{1,0:T(8,128)(2,1)}) fusion(bf16[4096,2432]{1,0:T(8,128)(2,1)} %add_convert_fusion.2, bf16[4096,2432]{1,0:T(8,128)(2,1)} %get-tuple-element.72, f32[4096,2432]{1,0:T(8,128)} %fusion.62, bf16[4096,1792]{1,0:T(8,128)(2,1)} %bitcast.79, bf16[2432,1792]{1,0:T(8,128)(2,1)} %collective-permute-done.9), kind=kOutput, calls=%fused_computation.15 | convolution fusion | flops 35891183616 | bytes 142934016 | tf_op jit(solution)/shard_map/dot_general | solution.py:29
  1009.4 46.7 %fusion.67 = f32[4096,1792]{1,0:T(8,128)} fusion(bf16[4096,2432]{1,0:T(8,128)(2,1)} %get-tuple-element.55, bf16[1792,4736]{1,0:T(8,128)(2,1)} %param.15), kind=kOutput, calls=%fused_computation.111 | convolution fusion | flops 35701915648 | bytes 57999360 | tf_op jit(solution)/shard_map/dot_general | solution.py:29
  1056.1 54.1 %add_add_fusion = f32[4096,1792]{1,0:T(8,128)} fusion(f32[4096,1792]{1,0:T(8,128)} %fusion.75, f32[4096,1792]{1,0:T(8,128)} %fusion.67, bf16[4096,2432]{1,0:T(8,128)(2,1)} %get-tuple-element.57, bf16[1792,4736]{1,0:T(8,128)(2,1)} %param.16), kind=kOutput, calls=%fused_computation.48 | convolution fusion | flops 35716595712 | bytes 116719616 | tf_op jit(solution)/shard_map/dot_general | solution.py:29
  1110.1 44.2 %add_convert_fusion.5 = bf16[4096,2304]{1,0:T(8,128)(2,1)} fusion(f32[4096,2304]{1,0:T(8,128)} %fusion.56, bf16[4096,1792]{1,0:T(8,128)(2,1)} %bitcast.71, bf16[1792,2304]{1,0:T(8,128)(2,1)} %collective-permute-done.8), kind=kOutput, calls=%fused_computation.47 | convolution fusion | flops 33841741824 | bytes 79560704 | tf_op jit(solution)/shard_map/dot_general | solution.py:25
  1154.4 106.2 %collective-permute-done.10 = bf16[1792,2304]{1,0:T(8,128)(2,1)} collective-permute-done((bf16[1792,2304]{1,0:T(8,128)(2,1)}, bf16[1792,2304]{1,0:T(8,128)(2,1)}, u32[]{:S(2)}, u32[]{:S(2)}) %collective-permute-start.10) | collective-permute-done | bytes 8257568 | tf_op jit(solution)/shard_map/ppermute | solution.py:127
  1260.6 50.4 %fusion.20 = (bf16[4096,2304]{1,0:T(8,128)(2,1)}, bf16[4096,2304]{1,0:T(8,128)(2,1)}) fusion(bf16[4096,2304]{1,0:T(8,128)(2,1)} %add_convert_fusion.5, f32[4096,2304]{1,0:T(8,128)} %fusion.54, bf16[4096,1792]{1,0:T(8,128)(2,1)} %bitcast.72, bf16[1792,2304]{1,0:T(8,128)(2,1)} %collective-permute-done.10), kind=kOutput, calls=%fused_computation.37 | convolution fusion | flops 33917239296 | bytes 117309440 | tf_op jit(solution)/shard_map/dot_general | solution.py:25
  1311.0 43.4 %convolution_add_fusion.1 = f32[4096,1792]{1,0:T(8,128)} fusion(f32[4096,1792]{1,0:T(8,128)} %convolution_add_fusion.2, bf16[4096,2304]{1,0:T(8,128)(2,1)} %get-tuple-element.48, bf16[4736,1792]{1,0:T(8,128)(2,1)} %param.17), kind=kOutput, calls=%fused_computation.50 | convolution fusion | flops 33830207488 | bytes 85852160 | tf_op jit(solution)/shard_map/dot_general | solution.py:25
  1363.2 90.2 %fusion.8 = f32[4736,1792]{1,0:T(8,128)} fusion(bf16[4096,1792]{1,0:T(8,128)(2,1)} %bitcast.77, bf16[4096,2304]{1,0:T(8,128)(2,1)} %get-tuple-element.48, bf16[4096,2432]{1,0:T(8,128)(2,1)} %get-tuple-element.47), kind=kOutput, calls=%fused_computation.25 | convolution fusion | flops 69602377728 | bytes 87425024 | tf_op jit(solution)/shard_map/dot_general | solution.py:33
  1453.4 85.5 %collective-permute-done.12 = bf16[2304,1792]{1,0:T(8,128)(2,1)} collective-permute-done((bf16[2304,1792]{1,0:T(8,128)(2,1)}, bf16[2304,1792]{1,0:T(8,128)(2,1)}, u32[]{:S(2)}, u32[]{:S(2)}) %collective-permute-start.12) | collective-permute-done | bytes 8257568 | tf_op jit(solution)/shard_map/ppermute | solution.py:127
  1539.0 57.8 %fusion.27 = (bf16[4096,2304]{1,0:T(8,128)(2,1)}, bf16[4096,2304]{1,0:T(8,128)(2,1)}) fusion(bf16[4096,2304]{1,0:T(8,128)(2,1)} %add_convert_fusion.5, bf16[4096,2304]{1,0:T(8,128)(2,1)} %get-tuple-element.74, f32[4096,2304]{1,0:T(8,128)} %fusion.59, bf16[4096,1792]{1,0:T(8,128)(2,1)} %bitcast.80, bf16[2304,1792]{1,0:T(8,128)(2,1)} %collective-permute-done.12), kind=kOutput, calls=%fused_computation.44 | convolution fusion | flops 34002173952 | bytes 136183808 | tf_op jit(solution)/shard_map/dot_general | solution.py:29
  1709.8 85.2 %fusion.16 = f32[1792,4736]{1,0:T(8,128)} fusion(bf16[4096,1792]{1,0:T(8,128)(2,1)} %bitcast.63, bf16[4096,2304]{1,0:T(8,128)(2,1)} %get-tuple-element.58, bf16[4096,2432]{1,0:T(8,128)(2,1)} %get-tuple-element.57), kind=kOutput, calls=%fused_computation.33 | convolution fusion | flops 69602377728 | bytes 87425024 | tf_op jit(solution)/shard_map/dot_general | solution.py:33
  1799.7 85.4 %fusion.12 = f32[1792,4736]{1,0:T(8,128)} fusion(bf16[4096,1792]{1,0:T(8,128)(2,1)} %bitcast.64, bf16[4096,2304]{1,0:T(8,128)(2,1)} %get-tuple-element.56, bf16[4096,2432]{1,0:T(8,128)(2,1)} %get-tuple-element.55), kind=kOutput, calls=%fused_computation.29 | convolution fusion | flops 69602377728 | bytes 87425024 | tf_op jit(solution)/shard_map/dot_general | solution.py:33
  (130 shorter events, 447.6 us)
Async XLA Ops:
  7.2 193.1 %all-gather.5.cloned.1.call-start = ((), (), s32[]{:S(2)}) async-start(), calls=%async_computation.3 | async-start | bytes 18350080 | tf_op jit(solution)/shard_map/all_gather | solution.py:146
  14.7 43.4 %collective-permute-start = (bf16[2,256,1792]{2,1,0:T(8,128)(2,1)S(1)}, bf16[2,256,1792]{2,1,0:T(8,128)(2,1)S(1)}, u32[]{:S(2)}, u32[]{:S(2)}) collective-permute-start(bf16[2,256,1792]{2,1,0:T(8,128)(2,1)S(1)} %get-tuple-element.69), channel_id=1, source_target_pairs={{0,4},{4,0},{1,5},{5,1},{2,6},{6,2},{3,7},{7,3}} | collective-permute-start | bytes 5505032 | tf_op jit(solution)/shard_map/ppermute | solution.py:127
  60.3 235.9 %all-gather.7.cloned.1.call-start = ((), (), s32[]{:S(2)}) async-start(), calls=%async_computation.4 | async-start | bytes 18350080 | tf_op jit(solution)/shard_map/all_gather | solution.py:147
  60.3 41.4 %collective-permute-start.1 = (bf16[2,256,1792]{2,1,0:T(8,128)(2,1)}, bf16[2,256,1792]{2,1,0:T(8,128)(2,1)S(1)}, u32[]{:S(2)}, u32[]{:S(2)}) collective-permute-start(bf16[2,256,1792]{2,1,0:T(8,128)(2,1)} %copy-done.6), channel_id=1, source_target_pairs={{0,4},{4,0},{1,5},{5,1},{2,6},{6,2},{3,7},{7,3}} | collective-permute-start | bytes 5505032 | tf_op jit(solution)/shard_map/ppermute | solution.py:127
  103.9 334.0 %all-gather.9.cloned.1.call-start = ((), (), s32[]{:S(2)}) async-start(), calls=%async_computation.5 | async-start | bytes 18350080 | tf_op jit(solution)/shard_map/all_gather | solution.py:146
  106.3 40.4 %collective-permute-start.3 = (bf16[2,256,1792]{2,1,0:T(8,128)(2,1)S(1)}, bf16[2,256,1792]{2,1,0:T(8,128)(2,1)S(1)}, u32[]{:S(2)}, u32[]{:S(2)}) collective-permute-start(bf16[2,256,1792]{2,1,0:T(8,128)(2,1)S(1)} %get-tuple-element.68), channel_id=1, source_target_pairs={{0,4},{4,0},{1,5},{5,1},{2,6},{6,2},{3,7},{7,3}} | collective-permute-start | bytes 5505032 | tf_op jit(solution)/shard_map/ppermute | solution.py:127
  148.9 357.7 %all-gather.11.cloned.1.call-start = ((), (), s32[]{:S(2)}) async-start(), calls=%async_computation.6 | async-start | bytes 18350080 | tf_op jit(solution)/shard_map/all_gather | solution.py:147
  149.0 47.2 %collective-permute-start.4 = (bf16[2,256,1792]{2,1,0:T(8,128)(2,1)}, bf16[2,256,1792]{2,1,0:T(8,128)(2,1)}, u32[]{:S(2)}, u32[]{:S(2)}) collective-permute-start(bf16[2,256,1792]{2,1,0:T(8,128)(2,1)} %copy-done.5), channel_id=1, source_target_pairs={{0,4},{4,0},{1,5},{5,1},{2,6},{6,2},{3,7},{7,3}} | collective-permute-start | bytes 5505032 | tf_op jit(solution)/shard_map/ppermute | solution.py:127
  150.2 144.1 %collective-permute-start.2 = (bf16[1792,1152]{1,0:T(8,128)(2,1)}, bf16[1792,1152]{1,0:T(8,128)(2,1)}, u32[]{:S(2)}, u32[]{:S(2)}) collective-permute-start(bf16[1792,1152]{1,0:T(8,128)(2,1)} %param.13), channel_id=1, source_target_pairs={{0,4},{4,0},{1,5},{5,1},{2,6},{6,2},{3,7},{7,3}} | collective-permute-start | bytes 12386312 | tf_op jit(solution)/shard_map/ppermute | solution.py:127
  151.0 333.8 %collective-permute-start.5 = (bf16[896,1792]{1,0:T(8,128)(2,1)}, bf16[896,1792]{1,0:T(8,128)(2,1)}, u32[]{:S(2)}, u32[]{:S(2)}) collective-permute-start(bf16[896,1792]{1,0:T(8,128)(2,1)} %param.14), channel_id=1, source_target_pairs={{0,4},{4,0},{1,5},{5,1},{2,6},{6,2},{3,7},{7,3}} | collective-permute-start | bytes 9633800 | tf_op jit(solution)/shard_map/ppermute | solution.py:127
  160.4 504.9 %collective-permute-start.6 = (bf16[1792,2432]{1,0:T(8,128)(2,1)}, bf16[1792,2432]{1,0:T(8,128)(2,1)}, u32[]{:S(2)}, u32[]{:S(2)}) collective-permute-start(bf16[1792,2432]{1,0:T(8,128)(2,1)} %slice.42), channel_id=1, source_target_pairs={{0,4},{4,0},{1,5},{5,1},{2,6},{6,2},{3,7},{7,3}} | collective-permute-start | bytes 26148872 | tf_op jit(solution)/shard_map/ppermute | solution.py:127
  169.9 634.4 %collective-permute-start.7 = (bf16[1792,2432]{1,0:T(8,128)(2,1)}, bf16[1792,2432]{1,0:T(8,128)(2,1)}, u32[]{:S(2)}, u32[]{:S(2)}) collective-permute-start(bf16[1792,2432]{1,0:T(8,128)(2,1)} %slice.43), channel_id=1, source_target_pairs={{0,4},{4,0},{1,5},{5,1},{2,6},{6,2},{3,7},{7,3}} | collective-permute-start | bytes 26148872 | tf_op jit(solution)/shard_map/ppermute | solution.py:127
  196.2 751.0 %collective-permute-start.9 = (bf16[2432,1792]{1,0:T(8,128)(2,1)}, bf16[2432,1792]{1,0:T(8,128)(2,1)}, u32[]{:S(2)}, u32[]{:S(2)}) collective-permute-start(bf16[2432,1792]{1,0:T(8,128)(2,1)} %slice.46), channel_id=1, source_target_pairs={{0,4},{4,0},{1,5},{5,1},{2,6},{6,2},{3,7},{7,3}} | collective-permute-start | bytes 26148872 | tf_op jit(solution)/shard_map/ppermute | solution.py:127
  200.0 1396.8 %reduce-scatter.4.cloned.1.call-start = ((), (), s32[]{:S(2)}) async-start(), calls=%async_computation.7 | async-start | bytes 36700160 | tf_op jit(solution)/shard_map/reduce_scatter | solution.py:198
  294.3 815.8 %collective-permute-start.8 = (bf16[1792,2304]{1,0:T(8,128)(2,1)}, bf16[1792,2304]{1,0:T(8,128)(2,1)}, u32[]{:S(2)}, u32[]{:S(2)}) collective-permute-start(bf16[1792,2304]{1,0:T(8,128)(2,1)} %slice.44), channel_id=1, source_target_pairs={{0,4},{4,0},{1,5},{5,1},{2,6},{6,2},{3,7},{7,3}} | collective-permute-start | bytes 24772616 | tf_op jit(solution)/shard_map/ppermute | solution.py:127
  484.8 775.7 %collective-permute-start.10 = (bf16[1792,2304]{1,0:T(8,128)(2,1)}, bf16[1792,2304]{1,0:T(8,128)(2,1)}, u32[]{:S(2)}, u32[]{:S(2)}) collective-permute-start(bf16[1792,2304]{1,0:T(8,128)(2,1)} %slice.45), channel_id=1, source_target_pairs={{0,4},{4,0},{1,5},{5,1},{2,6},{6,2},{3,7},{7,3}} | collective-permute-start | bytes 24772616 | tf_op jit(solution)/shard_map/ppermute | solution.py:127
  1354.4 440.7 %reduce-scatter.8.cloned.1.call-start = ((), (), s32[]{:S(2)}) async-start(), calls=%async_computation.9 | async-start | bytes 18350080 | tf_op jit(solution)/shard_map/reduce_scatter | solution.py:210
  1363.2 175.8 %collective-permute-start.12 = (bf16[2304,1792]{1,0:T(8,128)(2,1)}, bf16[2304,1792]{1,0:T(8,128)(2,1)}, u32[]{:S(2)}, u32[]{:S(2)}) collective-permute-start(bf16[2304,1792]{1,0:T(8,128)(2,1)} %slice.47), channel_id=1, source_target_pairs={{0,4},{4,0},{1,5},{5,1},{2,6},{6,2},{3,7},{7,3}} | collective-permute-start | bytes 24772616 | tf_op jit(solution)/shard_map/ppermute | solution.py:127
  1648.3 236.8 %reduce-scatter.6.cloned.1.call-start = ((), (), s32[]{:S(2)}) async-start(), calls=%async_computation.8 | async-start | bytes 18350080 | tf_op jit(solution)/shard_map/reduce_scatter | solution.py:211
  1709.0 182.8 %collective-permute-start.11 = (f32[2,256,1792]{2,1,0:T(8,128)}, f32[2,256,1792]{2,1,0:T(8,128)}, u32[]{:S(2)}, u32[]{:S(2)}) collective-permute-start(f32[2,256,1792]{2,1,0:T(8,128)} %get-tuple-element.64), channel_id=1, source_target_pairs={{0,4},{4,0},{1,5},{5,1},{2,6},{6,2},{3,7},{7,3}} | collective-permute-start | bytes 11010056 | tf_op jit(solution)/shard_map/ppermute | solution.py:127
  1798.5 89.0 %copy-start.11 = (f32[3584]{0:T(1024)S(1)}, f32[3584]{0:T(1024)}, u32[]{:S(2)}) copy-start(f32[3584]{0:T(1024)} %param.12) | copy-start | bytes 43012
  1798.5 93.3 %copy-start.13 = (f32[2,256]{1,0:T(2,128)S(1)}, f32[2,256]{1,0:T(2,128)}, u32[]{:S(2)}) copy-start(f32[2,256]{1,0:T(2,128)} %copy-done.12) | copy-start | bytes 6148
  1798.5 93.3 %copy-start.15 = (f32[2,256]{1,0:T(2,128)S(1)}, f32[2,256]{1,0:T(2,128)}, u32[]{:S(2)}) copy-start(f32[2,256]{1,0:T(2,128)} %copy-done.14) | copy-start | bytes 6148
  1798.5 89.0 %collective-permute-start.13 = (bf16[2,256,1792]{2,1,0:T(8,128)(2,1)}, bf16[2,256,1792]{2,1,0:T(8,128)(2,1)S(1)}, u32[]{:S(2)}, u32[]{:S(2)}) collective-permute-start(bf16[2,256,1792]{2,1,0:T(8,128)(2,1)} %convert_element_type.109), channel_id=1, source_target_pairs={{0,4},{4,0},{1,5},{5,1},{2,6},{6,2},{3,7},{7,3}} | collective-permute-start | bytes 5505032 | tf_op jit(solution)/shard_map/ppermute | solution.py:127
  (20 other events, 413.7 us)
Sparse Core Ops, SparseCore 0:
  60.4 92.3 all-gather.4
  154.9 91.1 all-gather.6
  248.3 91.1 all-gather.8
  341.5 91.1 all-gather.10
  1354.5 204.8 reduce-scatter.3
  1648.5 107.8 reduce-scatter.7
  1758.9 108.3 reduce-scatter.5
